TPU v7x, 256 devices: a whole 4x4x8 slice. The times are simulated.
256 devices in a mesh: dp: 8 (over z), task: 16 (over y, x), mp: 2 (over core).
Axes of the slice: x: 4, y: 4, z: 8, core: 2. Of those that a mesh axis runs over, the one named last changes fastest.
Arguments:
- deltas: bfloat16 [16, 2, 256, 28672], P('task', None, 'dp', 'mp'), may hold values from -3.984375 to 3.984375, as said below
- keep_blocks: int32 [16, 2, 2], P('task'), may hold values 0 or 1
- base_weights: bfloat16 [2, 256, 28672], P(None, 'dp', 'mp'), may hold values from -6 to 6
Outputs:
- merged: float32 [2, 256, 28672], P(None, 'dp', 'mp')
Inputs may be any that keep to these rules, and one draw needn't show every extreme that they name: `deltas`: every entry is a whole multiple of 1/64.
All inputs are finite; a program needn't handle non-finite values. No bound on the sum of `keep_blocks` on one device may be relied on, other than what follows from the above.
Results may differ from a plain program's by a relative error of at most 0.0003.
Values may be sent and summed in bfloat16 or wider, within the bound.
A program may use at most 128 MiB of HBM per device.

v0:
```python
import jax
import jax.numpy as jnp
from jax import lax
from jax.sharding import PartitionSpec as P

BLOCK = 128


def in_blocks(value, dim, devices):
    lengths = value.shape
    pieces = value.reshape(*lengths[:dim], devices, lengths[dim] // devices, *lengths[dim + 1 :])
    return jnp.moveaxis(pieces, dim, 0)


def cut_rows(length, count):
    unit = 8 if length >= 8 * count else 1
    return [length // unit * k // count * unit for k in range(1, count)]


def laid_out(pieces, dim):
    lengths = list(pieces.shape[1:])
    lengths[dim] *= pieces.shape[0]
    return jnp.moveaxis(pieces, 0, dim).reshape(lengths)


def exchange_in_pieces(value, axis, pieces, split_dim, concat_dim):
    blocks = in_blocks(value, split_dim, lax.axis_size(axis))
    widest = max(range(1, max(2, blocks.ndim - 1)), key=lambda d: blocks.shape[d])
    finished = []
    for slab in jnp.split(blocks, cut_rows(blocks.shape[widest], pieces), axis=widest):
        if slab.size:
            finished.append(lax.all_to_all(slab, axis, split_axis=0, concat_axis=0, tiled=True))
    return laid_out(jnp.concatenate(finished, axis=widest), concat_dim)


def combine(totals, own_base):
    upward, downward, up_count, down_count = totals
    elected = jnp.sign(upward + downward)
    upper_mean = upward / jnp.maximum(up_count, 1.0)
    lower_mean = downward / jnp.maximum(down_count, 1.0)
    agreed = jnp.where(elected > 0, upper_mean, jnp.where(elected < 0, lower_mean, 0.0))
    return own_base.astype(jnp.float32) + agreed


def statistics(trimmed):
    upward = jnp.maximum(trimmed, 0.0)
    downward = jnp.minimum(trimmed, 0.0)
    up_count = (trimmed > 0).astype(jnp.float32)
    down_count = (trimmed < 0).astype(jnp.float32)
    return (upward, downward, up_count, down_count)


def on_device(deltas, keep_blocks, base_weights):
    row_count = deltas.shape[2]
    block_count = keep_blocks.shape[2]
    row_start = lax.axis_index("dp") * row_count
    block_of_row = (row_start + jnp.arange(row_count, dtype=jnp.int32)) // BLOCK
    block_hits = (
        block_of_row[:, None] == jnp.arange(block_count, dtype=jnp.int32)[None, :]
    ).astype(jnp.float32)
    row_keep = jnp.dot(keep_blocks[0].astype(jnp.float32), block_hits.T)
    trimmed = deltas[0].astype(jnp.float32) * row_keep[:, :, None]
    share_rows = row_count // lax.axis_size("task")
    sendable = trimmed.astype(jnp.bfloat16)[None]
    arrived = exchange_in_pieces(sendable, "task", 2, 2, 0)
    upward, downward, up_count, down_count = statistics(arrived.astype(jnp.float32))
    totals = (
        jnp.sum(upward, axis=0),
        jnp.sum(downward, axis=0),
        jnp.sum(up_count, axis=0),
        jnp.sum(down_count, axis=0),
    )
    own_base = lax.dynamic_slice_in_dim(
        base_weights, lax.axis_index("task") * share_rows, share_rows, 1
    )
    merged_part = combine(totals, own_base)
    return lax.all_gather(merged_part, "task", axis=1, tiled=True)


def solution(mesh):
    in_specs = (P("task", None, "dp", "mp"), P("task", None, None), P(None, "dp", "mp"))
    out_specs = P(None, "dp", "mp")
    return jax.shard_map(
        on_device, mesh=mesh, in_specs=in_specs, out_specs=out_specs, check_vma=False
    )
```

profile of v0, /device:TPU:1, one launch (start us, length us, event | category | flops | bytes accessed | tf_op | source)
XLA Modules:
  0.0 137.9 jit_solution(14409906547524525671)
XLA Ops:
  6.5 0.9 convolution_bitcast_fusion
  7.4 0.1 copy.19
  7.5 3.4 %copy.13 = f32[1,2,32,14336]{3,1,2,0:T(2,128)S(1)} copy(bf16[1,2,32,14336]{3,2,1,0:T(8,128)(2,1)} %param.3) | data formatting | bytes 5505024 | tf_op jit(solution)/shard_map/convert_element_type | solution.py:62
  10.9 1.6 %fusion.4 = bf16[16,1,2,2,14336]{4,2,3,0,1:T(2,128)(2,1)S(1)} fusion(f32[1,2,16,2,14336]{4,1,3,2,0:T(2,128)S(1)} %bitcast.9, f32[2,16,2]{0,2,1:T(2,128)S(1)} %bitcast.10), kind=kLoop, calls=%fused_computation.9 | loop fusion | flops 1835008 | bytes 5505280 | tf_op jit(solution)/shard_map/transpose | solution.py:12
  12.5 3.9 %fusion.8 = (bf16[16,1,1,2,14336]{4,2,3,0,1:T(2,128)(2,1)S(1)}, bf16[16,1,1,2,14336]{4,2,3,0,1:T(2,128)(2,1)S(1)}) fusion(bf16[16,1,2,2,14336]{4,2,3,0,1:T(2,128)(2,1)S(1)} %fusion.4), kind=kLoop, calls=%fused_computation.24 | loop fusion | bytes 3670016 | tf_op jit(solution)/shard_map/split | solution.py:30
  16.4 1.9 %copy.15 = bf16[16,1,1,2,14336]{4,3,2,1,0:T(2,128)(2,1)} copy(bf16[16,1,1,2,14336]{4,2,3,0,1:T(2,128)(2,1)S(1)} %get-tuple-element.9) | data formatting | bytes 1835008 | tf_op jit(solution)/shard_map/split | solution.py:30
  18.3 7.6 %all-to-all-start = ((bf16[16,1,1,2,14336]{4,3,2,1,0:T(2,128)(2,1)}), bf16[16,1,1,2,14336]{4,3,2,1,0:T(2,128)(2,1)S(1)}, u32[]{:S(2)}, u32[]{:S(2)}) async-start(bf16[16,1,1,2,14336]{4,3,2,1,0:T(2,128)(2,1)} %copy.15), calls=%async_computation | async-start | bytes 1835008 | tf_op jit(solution)/shard_map/all_to_all | solution.py:32
  25.9 1.9 %copy.16 = bf16[16,1,1,2,14336]{4,3,2,1,0:T(2,128)(2,1)} copy(bf16[16,1,1,2,14336]{4,2,3,0,1:T(2,128)(2,1)S(1)} %get-tuple-element.10) | data formatting | bytes 1835008 | tf_op jit(solution)/shard_map/split | solution.py:30
  27.8 12.8 %all-to-all-done = bf16[16,1,1,2,14336]{4,3,2,1,0:T(2,128)(2,1)S(1)} async-done(((bf16[16,1,1,2,14336]{4,3,2,1,0:T(2,128)(2,1)}), bf16[16,1,1,2,14336]{4,3,2,1,0:T(2,128)(2,1)S(1)}, u32[]{:S(2)}, u32[]{:S(2)}) %all-to-all-start) | async-done | bytes 917536 | tf_op jit(solution)/shard_map/all_to_all | solution.py:32
  40.5 4.0 %all-to-all-start.1 = ((bf16[16,1,1,2,14336]{4,3,2,1,0:T(2,128)(2,1)}), bf16[16,1,1,2,14336]{4,3,2,1,0:T(2,128)(2,1)S(1)}, u32[]{:S(2)}, u32[]{:S(2)}) async-start(bf16[16,1,1,2,14336]{4,3,2,1,0:T(2,128)(2,1)} %copy.16), calls=%async_computation.1 | async-start | bytes 1835008 | tf_op jit(solution)/shard_map/all_to_all | solution.py:32
  44.5 0.2 all-gather.2.cloned.1.call-start
  44.7 13.6 %all-to-all-done.1 = bf16[16,1,1,2,14336]{4,3,2,1,0:T(2,128)(2,1)S(1)} async-done(((bf16[16,1,1,2,14336]{4,3,2,1,0:T(2,128)(2,1)}), bf16[16,1,1,2,14336]{4,3,2,1,0:T(2,128)(2,1)S(1)}, u32[]{:S(2)}, u32[]{:S(2)}) %all-to-all-start.1) | async-done | bytes 917536 | tf_op jit(solution)/shard_map/all_to_all | solution.py:32
  58.3 8.4 %fusion.2 = (f32[2,2,14336]{2,1,0:T(2,128)S(1)}, f32[2,2,14336]{2,1,0:T(2,128)S(1)}, f32[2,2,14336]{2,1,0:T(2,128)S(1)}, f32[2,2,14336]{2,1,0:T(2,128)S(1)}) fusion(bf16[16,1,1,2,14336]{4,3,2,1,0:T(2,128)(2,1)S(1)} %all-to-all-done.1, bf16[16,1,1,2,14336]{4,3,2,1,0:T(2,128)(2,1)S(1)} %all-to-all-done), kind=kLoop, calls=%fused_computation.6 | loop fusion | flops 10780672 | bytes 2752512 | tf_op jit(solution)/shard_map/reduce_sum | solution.py:70
  66.7 1.7 %convert_add_fusion = f32[2,2,14336]{2,1,0:T(2,128)S(1)} fusion(f32[2,2,14336]{2,1,0:T(2,128)S(1)} %get-tuple-element.6, f32[2,2,14336]{2,1,0:T(2,128)S(1)} %get-tuple-element.7, f32[2,2,14336]{2,1,0:T(2,128)S(1)} %get-tuple-element.8, f32[2,2,14336]{2,1,0:T(2,128)S(1)} %get-tuple-element.5, bf16[2,32,14336]{2,1,0:T(8,128)(2,1)} %param.5, s32[]{:T(128)S(6)} %select_n.20), kind=kLoop, calls=%fused_computation.15 | loop fusion | flops 688128 | bytes 1261572 | tf_op jit(solution)/shard_map/add | solution.py:42
  68.4 0.9 copy.17
  69.2 0.0 all-gather.2.cloned.1.call-update
  69.2 55.8 %all-gather.2.cloned.1.call-done = f32[2,32,14336]{2,0,1:T(2,128)} async-done(((f32[2,2,14336]{2,0,1:T(2,128)}), f32[2,32,14336]{2,0,1:T(2,128)}) %all-gather.2.cloned.1.call-update) | async-done | bytes 3670032 | tf_op jit(solution)/shard_map/all_gather | solution.py:77
  125.1 6.0 %copy.18 = f32[2,32,14336]{2,1,0:T(8,128)} copy(f32[2,32,14336]{2,0,1:T(2,128)} %all-gather.2.cloned.1.call-done) | data formatting | bytes 7340032 | tf_op jit(solution)/shard_map/all_gather | solution.py:77
  (1 shorter events, 0.0 us)
Async XLA Ops:
  18.3 22.2 %all-to-all-start = ((bf16[16,1,1,2,14336]{4,3,2,1,0:T(2,128)(2,1)}), bf16[16,1,1,2,14336]{4,3,2,1,0:T(2,128)(2,1)S(1)}, u32[]{:S(2)}, u32[]{:S(2)}) async-start(bf16[16,1,1,2,14336]{4,3,2,1,0:T(2,128)(2,1)} %copy.15), calls=%async_computation | async-start | bytes 1835008 | tf_op jit(solution)/shard_map/all_to_all | solution.py:32
  40.5 17.8 %all-to-all-start.1 = ((bf16[16,1,1,2,14336]{4,3,2,1,0:T(2,128)(2,1)}), bf16[16,1,1,2,14336]{4,3,2,1,0:T(2,128)(2,1)S(1)}, u32[]{:S(2)}, u32[]{:S(2)}) async-start(bf16[16,1,1,2,14336]{4,3,2,1,0:T(2,128)(2,1)} %copy.16), calls=%async_computation.1 | async-start | bytes 1835008 | tf_op jit(solution)/shard_map/all_to_all | solution.py:32
  44.5 80.6 %all-gather.2.cloned.1.call-start = ((), (), s32[]{:S(2)}) async-start(), calls=%async_computation.2 | async-start | bytes 3899392 | tf_op jit(solution)/shard_map/all_gather | solution.py:77
Sparse Core Ops, SparseCore 0:
  69.4 55.6 all-gather.1
where the time goes:
time: 138 us
  waiting for transfers between devices  82.2 us (60%)
  local copies, waits for them, and re-layouts  18 us (13%)
  between operations  13.5 us (10%)
  starting transfers between devices  11.8 us (9%)
  other arithmetic  11.7 us (8%)
    all_gather x1, waiting for transfers between devices, on_device(): return lax.all_gather(merged_part, 'task', axis=1, tiled=True)  55.8 us
    all_to_all x2, waiting for transfers between devices, exchange_in_pieces(): lax.all_to_all(slab, axis, split_axis=0, concat_axis=0, tiled=True)  26.3 us
    all_to_all x2, starting transfers between devices, exchange_in_pieces(): lax.all_to_all(slab, axis, split_axis=0, concat_axis=0, tiled=True)  11.5 us
    reduce_sum x1, other arithmetic, on_device(): jnp.sum(up_count, axis=0)  8.36 us
    split x3, local copies, waits for them, and re-layouts, exchange_in_pieces(): jnp.split(blocks, cut_rows(blocks.shape[widest], pieces), axis=widest)  7.63 us
    all_gather x1, local copies, waits for them, and re-layouts, on_device(): return lax.all_gather(merged_part, 'task', axis=1, tiled=True)  6 us
    convert_element_type x1, local copies, waits for them, and re-layouts, on_device(): trimmed = deltas[0].astype(jnp.float32) * row_keep[:, :, None]  3.39 us
  transfers between devices with their start and end apart: 3, of which 3 were waited for; matrix products, arithmetic and copies ran while one was open for 1% of the time, Pallas kernels for 0%

commit v1 on v0

--- a/solution.py
+++ b/solution.py
@@ -4,6 +4,11 @@
 from jax.sharding import PartitionSpec as P
 
 BLOCK = 128
+
+
+def gather_from_all(shard, axis, dim):
+    copies = jnp.concatenate([shard] * lax.axis_size(axis), axis=dim)
+    return lax.all_to_all(copies, axis, dim, dim, tiled=True)
 
 
 def in_blocks(value, dim, devices):
@@ -74,7 +79,7 @@
         base_weights, lax.axis_index("task") * share_rows, share_rows, 1
     )
     merged_part = combine(totals, own_base)
-    return lax.all_gather(merged_part, "task", axis=1, tiled=True)
+    return gather_from_all(merged_part, "task", 1)
 
 
 def solution(mesh):

time: 138 us -> 128 us (0.928); the launches traced: 138 us -> 126 us
  waiting for transfers between devices: 82.2 us -> 26.6 us
  blocking collectives: 0 us -> 48.1 us
  between operations: 13.5 us -> 0.06 us
  local copies, waits for them, and re-layouts: 18 us -> 27.6 us
    all_gather x1 -> x0, waiting for transfers between devices: 55.8 us -> none  [on_device(): return lax.all_gather(merged_part, 'task', axis=1, tiled=True)]
    all_to_all x0 -> x1, blocking collectives: none -> 48.1 us  [gather_from_all(): return lax.all_to_all(copies, axis, dim, dim, tiled=True)]
    concatenate x0 -> x2, local copies, waits for them, and re-layouts: none -> 12.5 us  [gather_from_all(): copies = jnp.concatenate([shard] * lax.axis_size(axis), axis=dim)]
    all_gather x1 -> x0, local copies, waits for them, and re-layouts: 6 us -> none  [on_device(): return lax.all_gather(merged_part, 'task', axis=1, tiled=True)]
    all_to_all x0 -> x1, local copies, waits for them, and re-layouts: none -> 3.96 us  [gather_from_all(): return lax.all_to_all(copies, axis, dim, dim, tiled=True)]
  transfers between devices with their start and end apart: 3 -> 2, of which waited for: 3 -> 2; matrix products, arithmetic and copies ran while one was open for 1% -> 1% of each run, Pallas kernels for 0% -> 0%
where the time goes in v1:
time: 128 us; the launch traced here: 126 us
  blocking collectives  48.1 us (38%)
  local copies, waits for them, and re-layouts  27.6 us (22%)
  waiting for transfers between devices  26.6 us (21%)
  other arithmetic  11.7 us (9%)
  starting transfers between devices  11.5 us (9%)
    all_to_all x1, blocking collectives, gather_from_all(): return lax.all_to_all(copies, axis, dim, dim, tiled=True)  48.1 us
    all_to_all x2, waiting for transfers between devices, exchange_in_pieces(): lax.all_to_all(slab, axis, split_axis=0, concat_axis=0, tiled=True)  26.6 us
    concatenate x2, local copies, waits for them, and re-layouts, gather_from_all(): copies = jnp.concatenate([shard] * lax.axis_size(axis), axis=dim)  12.5 us
    all_to_all x2, starting transfers between devices, exchange_in_pieces(): lax.all_to_all(slab, axis, split_axis=0, concat_axis=0, tiled=True)  11.5 us
    reduce_sum x1, other arithmetic, on_device(): jnp.sum(up_count, axis=0)  8.36 us
    split x3, local copies, waits for them, and re-layouts, exchange_in_pieces(): jnp.split(blocks, cut_rows(blocks.shape[widest], pieces), axis=widest)  7.63 us
    all_to_all x1, local copies, waits for them, and re-layouts, gather_from_all(): return lax.all_to_all(copies, axis, dim, dim, tiled=True)  3.96 us
    convert_element_type x1, local copies, waits for them, and re-layouts, on_device(): trimmed = deltas[0].astype(jnp.float32) * row_keep[:, :, None]  3.39 us
  transfers between devices with their start and end apart: 2, of which 2 were waited for; matrix products, arithmetic and copies ran while one was open for 1% of the time, Pallas kernels for 0%

profile of v1, /device:TPU:1, one launch (start us, length us, event | category | flops | bytes accessed | tf_op | source)
XLA Modules:
  0.0 126.4 jit_solution(18187136601568411969)
XLA Ops:
  0.0 0.9 convolution_bitcast_fusion
  0.9 0.1 copy.19
  1.0 3.4 %copy.13 = f32[1,2,32,14336]{3,1,2,0:T(2,128)S(1)} copy(bf16[1,2,32,14336]{3,2,1,0:T(8,128)(2,1)} %param.3) | data formatting | bytes 5505024 | tf_op jit(solution)/shard_map/convert_element_type | solution.py:67
  4.4 1.6 %fusion.4 = bf16[16,1,2,2,14336]{4,2,3,0,1:T(2,128)(2,1)S(1)} fusion(f32[1,2,16,2,14336]{4,1,3,2,0:T(2,128)S(1)} %bitcast.9, f32[2,16,2]{0,2,1:T(2,128)S(1)} %bitcast.10), kind=kLoop, calls=%fused_computation.9 | loop fusion | flops 1835008 | bytes 5505280 | tf_op jit(solution)/shard_map/transpose | solution.py:17
  6.0 3.9 %fusion.8 = (bf16[16,1,1,2,14336]{4,2,3,0,1:T(2,128)(2,1)S(1)}, bf16[16,1,1,2,14336]{4,2,3,0,1:T(2,128)(2,1)S(1)}) fusion(bf16[16,1,2,2,14336]{4,2,3,0,1:T(2,128)(2,1)S(1)} %fusion.4), kind=kLoop, calls=%fused_computation.24 | loop fusion | bytes 3670016 | tf_op jit(solution)/shard_map/split | solution.py:35
  9.9 1.9 %copy.15 = bf16[16,1,1,2,14336]{4,3,2,1,0:T(2,128)(2,1)} copy(bf16[16,1,1,2,14336]{4,2,3,0,1:T(2,128)(2,1)S(1)} %get-tuple-element.9) | data formatting | bytes 1835008 | tf_op jit(solution)/shard_map/split | solution.py:35
  11.8 7.6 %all-to-all-start = ((bf16[16,1,1,2,14336]{4,3,2,1,0:T(2,128)(2,1)}), bf16[16,1,1,2,14336]{4,3,2,1,0:T(2,128)(2,1)S(1)}, u32[]{:S(2)}, u32[]{:S(2)}) async-start(bf16[16,1,1,2,14336]{4,3,2,1,0:T(2,128)(2,1)} %copy.15), calls=%async_computation | async-start | bytes 1835008 | tf_op jit(solution)/shard_map/all_to_all | solution.py:37
  19.4 1.9 %copy.16 = bf16[16,1,1,2,14336]{4,3,2,1,0:T(2,128)(2,1)} copy(bf16[16,1,1,2,14336]{4,2,3,0,1:T(2,128)(2,1)S(1)} %get-tuple-element.10) | data formatting | bytes 1835008 | tf_op jit(solution)/shard_map/split | solution.py:35
  21.2 12.8 %all-to-all-done = bf16[16,1,1,2,14336]{4,3,2,1,0:T(2,128)(2,1)S(1)} async-done(((bf16[16,1,1,2,14336]{4,3,2,1,0:T(2,128)(2,1)}), bf16[16,1,1,2,14336]{4,3,2,1,0:T(2,128)(2,1)S(1)}, u32[]{:S(2)}, u32[]{:S(2)}) %all-to-all-start) | async-done | bytes 917536 | tf_op jit(solution)/shard_map/all_to_all | solution.py:37
  34.0 4.0 %all-to-all-start.1 = ((bf16[16,1,1,2,14336]{4,3,2,1,0:T(2,128)(2,1)}), bf16[16,1,1,2,14336]{4,3,2,1,0:T(2,128)(2,1)S(1)}, u32[]{:S(2)}, u32[]{:S(2)}) async-start(bf16[16,1,1,2,14336]{4,3,2,1,0:T(2,128)(2,1)} %copy.16), calls=%async_computation.1 | async-start | bytes 1835008 | tf_op jit(solution)/shard_map/all_to_all | solution.py:37
  38.0 13.8 %all-to-all-done.1 = bf16[16,1,1,2,14336]{4,3,2,1,0:T(2,128)(2,1)S(1)} async-done(((bf16[16,1,1,2,14336]{4,3,2,1,0:T(2,128)(2,1)}), bf16[16,1,1,2,14336]{4,3,2,1,0:T(2,128)(2,1)S(1)}, u32[]{:S(2)}, u32[]{:S(2)}) %all-to-all-start.1) | async-done | bytes 917536 | tf_op jit(solution)/shard_map/all_to_all | solution.py:37
  51.8 8.4 %fusion.2 = (f32[2,2,14336]{2,1,0:T(2,128)S(1)}, f32[2,2,14336]{2,1,0:T(2,128)S(1)}, f32[2,2,14336]{2,1,0:T(2,128)S(1)}, f32[2,2,14336]{2,1,0:T(2,128)S(1)}) fusion(bf16[16,1,1,2,14336]{4,3,2,1,0:T(2,128)(2,1)S(1)} %all-to-all-done.1, bf16[16,1,1,2,14336]{4,3,2,1,0:T(2,128)(2,1)S(1)} %all-to-all-done), kind=kLoop, calls=%fused_computation.6 | loop fusion | flops 10780672 | bytes 2752512 | tf_op jit(solution)/shard_map/reduce_sum | solution.py:75
  60.1 1.7 %convert_add_fusion = f32[2,2,14336]{2,1,0:T(2,128)S(1)} fusion(f32[2,2,14336]{2,1,0:T(2,128)S(1)} %get-tuple-element.6, f32[2,2,14336]{2,1,0:T(2,128)S(1)} %get-tuple-element.7, f32[2,2,14336]{2,1,0:T(2,128)S(1)} %get-tuple-element.8, f32[2,2,14336]{2,1,0:T(2,128)S(1)} %get-tuple-element.5, bf16[2,32,14336]{2,1,0:T(8,128)(2,1)} %param.5, s32[]{:T(128)S(6)} %select_n.20), kind=kLoop, calls=%fused_computation.15 | loop fusion | flops 688128 | bytes 1261572 | tf_op jit(solution)/shard_map/add | solution.py:47
  61.8 7.6 %concatenate.7 = f32[2,32,14336]{2,1,0:T(8,128)} concatenate(f32[2,2,14336]{2,1,0:T(2,128)S(1)} %convert_add_fusion, f32[2,2,14336]{2,1,0:T(2,128)S(1)} %convert_add_fusion, f32[2,2,14336]{2,1,0:T(2,128)S(1)} %convert_add_fusion, f32[2,2,14336]{2,1,0:T(2,128)S(1)} %convert_add_fusion, f32[2,2,14336]{2,1,0:T(2,128)S(1)} %convert_add_fusion, f32[2,2,14336]{2,1,0:T(2,128)S(1)} %convert_add_fusion, ...), dimensions={1} | concatenate | bytes 7340032 | tf_op jit(solution)/shard_map/concatenate | solution.py:10
  69.5 4.9 %copy.17 = f32[2,32,14336]{2,0,1:T(2,128)S(1)} copy(f32[2,32,14336]{2,1,0:T(8,128)} %concatenate.7) | data formatting | bytes 7340032 | tf_op jit(solution)/shard_map/concatenate | solution.py:10
  74.3 48.1 %all_to_all.15 = f32[2,32,14336]{2,0,1:T(2,128)S(1)} all-to-all(f32[2,32,14336]{2,0,1:T(2,128)S(1)} %copy.17), channel_id=1, replica_groups=mesh['dp'=8,'task'=16,'mp'=2] {'task'}, dimensions={1} | all-to-all | bytes 7340032 | tf_op jit(solution)/shard_map/all_to_all | solution.py:11
  122.4 4.0 %copy.18 = f32[2,32,14336]{2,1,0:T(8,128)} copy(f32[2,32,14336]{2,0,1:T(2,128)S(1)} %all_to_all.15) | data formatting | bytes 7340032 | tf_op jit(solution)/shard_map/all_to_all | solution.py:11
  (1 shorter events, 0.0 us)
Async XLA Ops:
  11.8 22.2 %all-to-all-start = ((bf16[16,1,1,2,14336]{4,3,2,1,0:T(2,128)(2,1)}), bf16[16,1,1,2,14336]{4,3,2,1,0:T(2,128)(2,1)S(1)}, u32[]{:S(2)}, u32[]{:S(2)}) async-start(bf16[16,1,1,2,14336]{4,3,2,1,0:T(2,128)(2,1)} %copy.15), calls=%async_computation | async-start | bytes 1835008 | tf_op jit(solution)/shard_map/all_to_all | solution.py:37
  34.0 17.8 %all-to-all-start.1 = ((bf16[16,1,1,2,14336]{4,3,2,1,0:T(2,128)(2,1)}), bf16[16,1,1,2,14336]{4,3,2,1,0:T(2,128)(2,1)S(1)}, u32[]{:S(2)}, u32[]{:S(2)}) async-start(bf16[16,1,1,2,14336]{4,3,2,1,0:T(2,128)(2,1)} %copy.16), calls=%async_computation.1 | async-start | bytes 1835008 | tf_op jit(solution)/shard_map/all_to_all | solution.py:37
